TPU v7x, 256 devices: a 8x8x2 block of a 8x8x16 slice. The times are simulated.
256 devices in a mesh: groups: 2 (over z), expert: 64 (over y, x), tensor: 2 (over core).
Axes of the slice: x: 8, y: 8, z: 2, core: 2. Of those that a mesh axis runs over, the one named last changes fastest.
The devices are a block of a 8x8x16 slice.
Arguments:
- tokens: bfloat16 [1024, 6144], P(('groups', 'expert')), parts along dimension 0, may hold values from -6 to 6
- routes: int32 [1024, 2], P(('groups', 'expert')), parts along dimension 0, may hold values from 0 to 3, all different within a row; in each aligned block of 8 rows (0 to 7, 8 to 15, ...) at most 5 rows name the same one
- router_logits: float32 [1024, 4], P(('groups', 'expert')), parts along dimension 0, may hold values from -9 to 310
- gate_weight: bfloat16 [64, 6144, 512], P('expert', None, 'tensor'), may hold values from -0.078125 to 0.078125
- up_weight: bfloat16 [64, 6144, 512], P('expert', None, 'tensor'), may hold values from -0.078125 to 0.078125
- down_weight: bfloat16 [64, 512, 6144], P('expert', 'tensor'), may hold values from -0.0625 to 0.0625
Outputs:
- layer_out: bfloat16 [1024, 6144], P(('groups', 'expert'), 'tensor'), parts along dimension 0
There are 2 independent parts, one for each index of `groups`. A program takes and returns all parts, laid end to end along the dimension named above; an argument that names none is the same for every part. Nothing has to cross between parts.
Inputs may be any that keep to these rules, and one draw needn't show every extreme that they name: `routes`: each row names two different experts. In the rows of one index of expert (aligned blocks of 8 rows) no expert is named more than 5 times, and in every draw some block names some expert exactly 5 times.
All inputs are finite; a program needn't handle non-finite values.
Results may differ from a plain program's by a relative error of at most 0.0049.
Values may be sent and summed in bfloat16 or wider, within the bound.
A program may use at most 64 MiB of HBM per device.

v0:
```python
import jax
import jax.numpy as jnp
from jax import lax
from jax.sharding import PartitionSpec as P

CAP = 5


def in_blocks(value, dim, devices):
    shape = value.shape
    blocks = value.reshape(*shape[:dim], devices, shape[dim] // devices, *shape[dim + 1 :])
    return jnp.moveaxis(blocks, dim, 0)


def sent_and_summed(value, axis, dim):
    blocks = in_blocks(value, dim, lax.axis_size(axis))
    arrived = lax.all_to_all(blocks, axis, split_axis=0, concat_axis=0, tiled=True)
    return arrived.sum(axis=0)


def piece_ends(length, count):
    lap = length // count
    if lap >= 8:
        lap -= lap % 8
    return [lap * k for k in range(1, count)]


def joined_along(blocks, dim):
    blocks = jnp.moveaxis(blocks, 0, dim)
    shape = blocks.shape
    return blocks.reshape(*shape[:dim], shape[dim] * shape[dim + 1], *shape[dim + 2 :])


def exchange_in_pieces(value, axis, pieces, split_dim, concat_dim):
    blocks = in_blocks(value, split_dim, lax.axis_size(axis))
    widest = max(range(1, max(2, blocks.ndim - 1)), key=lambda d: blocks.shape[d])
    finished = []
    for share in jnp.split(blocks, piece_ends(blocks.shape[widest], pieces), axis=widest):
        if share.size:
            finished.append(lax.all_to_all(share, axis, split_axis=0, concat_axis=0, tiled=True))
    return joined_along(jnp.concatenate(finished, axis=widest), concat_dim)


def shards(tokens, routes, router_logits, gate_weight, up_weight, down_weight):
    local_tokens = tokens.shape[0]
    width = tokens.shape[1]
    experts = router_logits.shape[1]
    devices = lax.axis_size("expert")
    segments = devices // experts
    capacity = CAP
    expert_ids = jnp.arange(experts, dtype=jnp.int32)
    picked = jnp.take_along_axis(router_logits, routes, axis=1)
    route_weight = jax.nn.softmax(picked, axis=1)
    onehot = (routes[:, :, None] == expert_ids[None, None, :]).astype(jnp.int32)
    flat_hot = onehot.reshape(local_tokens * 2, experts)
    earlier = jnp.cumsum(flat_hot, axis=0) - flat_hot
    slot_index = jnp.sum(earlier * flat_hot, axis=1).reshape(local_tokens, 2)
    target = routes * capacity + slot_index
    cell_ids = jnp.arange(experts * capacity, dtype=jnp.int32)
    placed = target[:, :, None] == cell_ids[None, None, :]
    pick_matrix = jnp.any(placed, axis=1).astype(jnp.bfloat16)
    mix_matrix = jnp.sum(route_weight[:, :, None] * placed.astype(jnp.float32), axis=1)
    buffer = jnp.einsum(
        "tc,td->cd", pick_matrix, tokens, preferred_element_type=jnp.float32
    ).astype(jnp.bfloat16)
    buffer = buffer.reshape(experts, capacity, width)
    gate_local = gate_weight[0]
    up_local = up_weight[0]
    down_local = down_weight[0]
    outgoing = jnp.repeat(buffer, segments, axis=0)
    half_width = width // lax.axis_size("tensor")
    own_columns = lax.dynamic_slice_in_dim(
        outgoing, lax.axis_index("tensor") * half_width, half_width, 2
    )
    slot_rows = lax.all_gather(
        lax.all_to_all(own_columns, "expert", split_axis=0, concat_axis=0, tiled=True),
        "tensor",
        axis=2,
        tiled=True,
    )
    sources = slot_rows.shape[0]
    items = slot_rows.shape[1]
    flattened = slot_rows.reshape(sources * items, slot_rows.shape[2])
    gate_out = jnp.dot(flattened, gate_local, preferred_element_type=jnp.float32)
    up_out = jnp.dot(flattened, up_local, preferred_element_type=jnp.float32)
    hidden = (jax.nn.silu(gate_out) * up_out).astype(jnp.bfloat16)
    result = jnp.dot(hidden, down_local, preferred_element_type=jnp.float32)
    partial_out = result.reshape(sources, items, width)
    reduced = sent_and_summed(partial_out, "tensor", 2)
    returned = exchange_in_pieces(reduced, "expert", 2, 0, 0)
    columns_here = returned.shape[2]
    gathered_out = jnp.sum(returned.reshape(experts, segments, capacity, columns_here), axis=1)
    gathered_out = gathered_out.reshape(experts * capacity, columns_here)
    layer_out = jnp.dot(
        mix_matrix,
        gathered_out,
        precision=lax.Precision.HIGHEST,
        preferred_element_type=jnp.float32,
    )
    return layer_out.astype(jnp.bfloat16)


def solution(mesh):
    return jax.shard_map(
        shards,
        mesh=mesh,
        in_specs=(
            P(("groups", "expert"), None),
            P(("groups", "expert"), None),
            P(("groups", "expert"), None),
            P("expert", None, "tensor"),
            P("expert", None, "tensor"),
            P("expert", "tensor", None),
        ),
        out_specs=P(("groups", "expert"), "tensor"),
        check_vma=False,
    )
```

profile of v0, /device:TPU:514, one launch (start us, length us, event | category | flops | bytes accessed | tf_op | source)
XLA Modules:
  0.0 314.4 jit_solution(12775214072166252372)
XLA Ops:
  6.5 0.0 copy-start
  6.6 0.0 all-gather.2.cloned.1.call-start
  6.6 0.9 copy.70
  7.5 0.1 eq.29
  7.5 0.1 fusion.12
  7.6 0.2 select_reduce_fusion.1
  7.8 0.1 reshape.54
  7.9 0.1 copy.72
  8.0 0.1 fusion.11
  8.1 1.9 convolution_convert_fusion
  10.0 1.1 reshape.56
  11.1 0.8 broadcast_in_dim.2
  11.8 0.3 constant_dynamic-slice_fusion
  12.1 94.5 %all_to_all.20 = bf16[64,5,3072]{2,1,0:T(8,128)(2,1)} all-to-all(bf16[64,5,3072]{2,1,0:T(8,128)(2,1)S(1)} %constant_dynamic-slice_fusion), channel_id=1, replica_groups=mesh['groups'=2,'expert'=64,'tensor'=2] {'expert'}, dimensions={0} | all-to-all | bytes 3932160 | tf_op jit(solution)/shard_map/all_to_all | solution.py:76
  106.6 0.1 all-gather.2.cloned.1.call-update
  106.7 4.7 %copy.91 = bf16[6144,256]{1,0:T(8,128)(2,1)} copy(bf16[6144,256]{0,1:T(8,128)(2,1)} %bitcast.38) | data formatting | bytes 6291456 | tf_op jit(solution)/shard_map/dot_general | solution.py:87
  111.4 27.0 %all-gather.2.cloned.1.call-done = bf16[64,5,6144]{2,1,0:T(8,128)(2,1)} async-done(((bf16[64,5,3072]{2,1,0:T(8,128)(2,1)}), bf16[64,5,6144]{2,1,0:T(8,128)(2,1)}) %all-gather.2.cloned.1.call-update) | async-done | bytes 3932176 | tf_op jit(solution)/shard_map/all_gather | solution.py:75
  138.4 7.7 %reshape.58 = bf16[320,6144]{1,0:T(8,128)(2,1)} reshape(bf16[64,5,6144]{2,1,0:T(8,128)(2,1)} %all-gather.2.cloned.1.call-done) | data formatting | bytes 7864320 | tf_op jit(solution)/shard_map/reshape | solution.py:83
  146.1 0.0 copy-done
  146.1 0.0 copy-start.5
  146.1 0.0 copy-start.6
  146.1 3.4 %fusion.2 = f32[320,256]{1,0:T(8,128)S(1)} fusion(bf16[320,6144]{1,0:T(8,128)(2,1)} %reshape.58, bf16[1,6144,256]{2,1,0:T(8,128)(2,1)S(1)} %copy-done), kind=kOutput, calls=%fused_computation.7 | convolution fusion | flops 1006632960 | bytes 7405568 | tf_op jit(solution)/shard_map/dot_general | solution.py:84
  149.6 0.0 copy-done.5
  149.6 0.8 copy-done.6
  150.4 0.0 copy-start.3
  150.4 1.8 fusion.7
  152.2 1.0 dot_general.24
  153.2 0.0 copy-done.3
  153.2 1.2 convolution_bitcast_fusion
  154.5 0.9 copy.81
  155.4 11.3 %all_to_all.21 = f32[2,64,5,3072]{3,1,2,0:T(8,128)} all-to-all(f32[2,64,5,3072]{3,1,2,0:T(8,128)S(1)} %copy.81), channel_id=1, replica_groups=mesh['groups'=2,'expert'=64,'tensor'=2] {'tensor'}, dimensions={0} | all-to-all | bytes 15728640 | tf_op jit(solution)/shard_map/all_to_all | solution.py:17
  166.8 6.3 %reduce_sum.48 = f32[64,5,3072]{2,0,1:T(8,128)} reduce(f32[2,64,5,3072]{3,1,2,0:T(8,128)} %all_to_all.21, f32[]{:T(128)} %constant.36.clone.1), dimensions={0}, to_apply=%region_6.7 | reduce | flops 983040 | bytes 11796484 | tf_op jit(solution)/shard_map/reduce_sum | solution.py:18
  173.0 1.5 split.8
  174.6 2.4 copy.83
  177.0 13.7 %all-to-all-start.2 = ((f32[64,1,2,3072]{3,2,1,0:T(2,128)}), f32[64,1,2,3072]{3,2,1,0:T(2,128)}, u32[]{:S(2)}, u32[]{:S(2)}) async-start(f32[64,1,2,3072]{3,2,1,0:T(2,128)} %copy.83), calls=%async_computation.2 | async-start | bytes 3145728 | tf_op jit(solution)/shard_map/all_to_all | solution.py:40
  190.7 1.9 split.9
  192.6 3.8 %copy.84 = f32[64,1,3,3072]{3,1,2,0:T(1,128)} copy(f32[64,1,3,3072]{3,0,2,1:T(8,128)S(1)} %split.9) | data formatting | bytes 4718592 | tf_op jit(solution)/shard_map/split | solution.py:38
  196.4 0.0 copy-start.2
  196.4 35.4 %all-to-all-done.2 = f32[64,1,2,3072]{3,2,1,0:T(2,128)} async-done(((f32[64,1,2,3072]{3,2,1,0:T(2,128)}), f32[64,1,2,3072]{3,2,1,0:T(2,128)}, u32[]{:S(2)}, u32[]{:S(2)}) %all-to-all-start.2) | async-done | bytes 1572896 | tf_op jit(solution)/shard_map/all_to_all | solution.py:40
  231.8 8.6 %all-to-all-start.3 = ((f32[64,1,3,3072]{3,1,2,0:T(1,128)}), f32[64,1,3,3072]{3,1,2,0:T(1,128)S(1)}, u32[]{:S(2)}, u32[]{:S(2)}) async-start(f32[64,1,3,3072]{3,1,2,0:T(1,128)} %copy.84), calls=%async_computation.3 | async-start | bytes 4718592 | tf_op jit(solution)/shard_map/all_to_all | solution.py:40
  240.4 0.1 copy.76
  240.5 0.1 copy.77
  240.6 0.1 reshape.61
  240.6 0.0 copy-done.2
  240.6 0.7 gather_fusion
  241.3 0.1 reshape.64
  241.4 0.1 fusion.15
  241.5 0.2 fusion.14
  241.7 0.1 fusion.13
  241.8 0.1 copy.78
  241.9 0.1 select_reduce_fusion
  242.0 3.1 copy.85
  245.0 51.5 %all-to-all-done.3 = f32[64,1,3,3072]{3,1,2,0:T(1,128)S(1)} async-done(((f32[64,1,3,3072]{3,1,2,0:T(1,128)}), f32[64,1,3,3072]{3,1,2,0:T(1,128)S(1)}, u32[]{:S(2)}, u32[]{:S(2)}) %all-to-all-start.3) | async-done | bytes 2359328 | tf_op jit(solution)/shard_map/all_to_all | solution.py:40
  296.5 0.0 copy-start.4
  296.5 0.4 copy.86
  296.9 1.0 copy-done.4
  297.9 0.0 copy-start.1
  297.9 2.3 pad_maximum_fusion
  300.3 3.6 %reduce_sum.49 = f32[4,5,3072]{2,0,1:T(4,128)} reduce(f32[4,16,5,3072]{3,1,0,2:T(8,128)} %bitcast.35, f32[]{:T(128)} %constant.36.clone.1), dimensions={1}, to_apply=%region_7.8 | reduce | flops 921600 | bytes 4177924 | tf_op jit(solution)/shard_map/reduce_sum | solution.py:92
  303.9 1.1 copy.87
  305.0 0.8 reshape.60
  305.7 1.9 convolution_convert_fusion.1
  307.6 0.0 copy-done.1
  (3 shorter events, 0.1 us)
Async XLA Ops:
  6.5 139.6 %copy-start = (bf16[1,6144,256]{2,1,0:T(8,128)(2,1)S(1)}, bf16[1,6144,256]{2,1,0:T(8,128)(2,1)}, u32[]{:S(2)}) copy-start(bf16[1,6144,256]{2,1,0:T(8,128)(2,1)} %param.9) | copy-start | bytes 9437188
  6.6 131.9 %all-gather.2.cloned.1.call-start = ((), (), s32[]{:S(2)}) async-start(), calls=%async_computation.4 | async-start | bytes 9437184 | tf_op jit(solution)/shard_map/all_gather | solution.py:75
  146.1 3.5 %copy-start.5 = (bf16[320,6144]{1,0:T(8,128)(2,1)S(1)}, bf16[320,6144]{1,0:T(8,128)(2,1)}, u32[]{:S(2)}) copy-start(bf16[320,6144]{1,0:T(8,128)(2,1)} %reshape.58) | copy-start | bytes 11796484
  146.1 4.3 %copy-start.6 = (bf16[1,6144,256]{2,1,0:T(8,128)(2,1)S(1)}, bf16[1,6144,256]{2,1,0:T(8,128)(2,1)}, u32[]{:S(2)}) copy-start(bf16[1,6144,256]{2,1,0:T(8,128)(2,1)} %param.10) | copy-start | bytes 9437188
  150.4 2.8 copy-start.3
  177.0 54.8 %all-to-all-start.2 = ((f32[64,1,2,3072]{3,2,1,0:T(2,128)}), f32[64,1,2,3072]{3,2,1,0:T(2,128)}, u32[]{:S(2)}, u32[]{:S(2)}) async-start(f32[64,1,2,3072]{3,2,1,0:T(2,128)} %copy.83), calls=%async_computation.2 | async-start | bytes 3145728 | tf_op jit(solution)/shard_map/all_to_all | solution.py:40
  196.4 44.2 %copy-start.2 = (f32[8,4]{0,1:T(4,128)S(1)}, f32[8,4]{0,1:T(4,128)}, u32[]{:S(2)}) copy-start(f32[8,4]{0,1:T(4,128)} %param.8) | copy-start | bytes 388
  231.8 64.7 %all-to-all-start.3 = ((f32[64,1,3,3072]{3,1,2,0:T(1,128)}), f32[64,1,3,3072]{3,1,2,0:T(1,128)S(1)}, u32[]{:S(2)}, u32[]{:S(2)}) async-start(f32[64,1,3,3072]{3,1,2,0:T(1,128)} %copy.84), calls=%async_computation.3 | async-start | bytes 4718592 | tf_op jit(solution)/shard_map/all_to_all | solution.py:40
  296.5 1.4 copy-start.4
  297.9 9.6 %copy-start.1 = (bf16[1,6144,256]{2,1,0:T(8,128)(2,1)S(1)}, bf16[1,6144,256]{2,1,0:T(8,128)(2,1)}, u32[]{:S(2)}) copy-start(bf16[1,6144,256]{2,1,0:T(8,128)(2,1)} %param.9) | copy-start | bytes 9437188
Sparse Core Ops, SparseCore 0:
  106.8 31.5 all-gather.1
where the time goes:
time: 315 us; the launch traced here: 314 us
  waiting for transfers between devices  114 us (36%)
  blocking collectives  106 us (34%)
  local copies, waits for them, and re-layouts  35.5 us (11%)
  starting transfers between devices  22.3 us (7%)
  between operations  13.6 us (4%)
  other arithmetic  13.1 us (4%)
  matrix products  10.2 us (3%)
    all_to_all x1, blocking collectives, shards(): lax.all_to_all(own_columns, 'expert', split_axis=0, concat_axis=0, tiled=...  94.5 us
    all_to_all x2, waiting for transfers between devices, exchange_in_pieces(): lax.all_to_all(share, axis, split_axis=0, concat_axis=0, tiled=True)  86.8 us
    all_gather x1, waiting for transfers between devices, shards(): lax.all_gather(lax.all_to_all(own_columns, 'expert', split_axis=0, concat...  27 us
    all_to_all x2, starting transfers between devices, exchange_in_pieces(): lax.all_to_all(share, axis, split_axis=0, concat_axis=0, tiled=True)  22.3 us
    all_to_all x1, blocking collectives, sent_and_summed(): lax.all_to_all(blocks, axis, split_axis=0, concat_axis=0, tiled=True)  11.3 us
    split x4, local copies, waits for them, and re-layouts, exchange_in_pieces(): jnp.split(blocks, piece_ends(blocks.shape[widest], pieces), axis=widest)  9.65 us
    reshape x1, local copies, waits for them, and re-layouts, shards(): flattened = slot_rows.reshape(sources * items, slot_rows.shape[2])  7.69 us
  transfers between devices with their start and end apart: 3, of which 3 were waited for; matrix products, arithmetic and copies ran while one was open for 5% of the time, Pallas kernels for 0%

commit v1 on v0

--- a/solution.py
+++ b/solution.py
@@ -72,11 +72,17 @@
     own_columns = lax.dynamic_slice_in_dim(
         outgoing, lax.axis_index("tensor") * half_width, half_width, 2
     )
-    slot_rows = lax.all_gather(
-        lax.all_to_all(own_columns, "expert", split_axis=0, concat_axis=0, tiled=True),
-        "tensor",
+    slot_rows = jnp.concatenate(
+        lax.all_to_all(
+            jnp.stack(
+                [lax.all_to_all(own_columns, "expert", split_axis=0, concat_axis=0, tiled=True)]
+                * lax.axis_size("tensor")
+            ),
+            "tensor",
+            0,
+            0,
+        ),
         axis=2,
-        tiled=True,
     )
     sources = slot_rows.shape[0]
     items = slot_rows.shape[1]

time: 315 us -> 301 us (0.956)
  the two profiles are of different devices: /device:TPU:514 before, /device:TPU:640 now
where the time goes in v1:
time: 301 us; the launch traced here: 300 us
  waiting for transfers between devices  157 us (52%)
  starting transfers between devices  62 us (21%)
  local copies, waits for them, and re-layouts  41.5 us (14%)
  blocking collectives  18.3 us (6%)
  other arithmetic  13.4 us (4%)
  matrix products  8.05 us (3%)
    all_to_all x2, waiting for transfers between devices, exchange_in_pieces(): lax.all_to_all(share, axis, split_axis=0, concat_axis=0, tiled=True)  85.8 us
    all_to_all x1, waiting for transfers between devices, shards(): lax.all_to_all(own_columns, 'expert', split_axis=0, concat_axis=0, tiled=...  71.2 us
    all_to_all x2, starting transfers between devices, exchange_in_pieces(): lax.all_to_all(share, axis, split_axis=0, concat_axis=0, tiled=True)  40.7 us
    all_to_all x1, starting transfers between devices, shards(): lax.all_to_all(own_columns, 'expert', split_axis=0, concat_axis=0, tiled=...  21.3 us
    all_to_all x1, blocking collectives, sent_and_summed(): lax.all_to_all(blocks, axis, split_axis=0, concat_axis=0, tiled=True)  11.3 us
    split x4, local copies, waits for them, and re-layouts, exchange_in_pieces(): jnp.split(blocks, piece_ends(blocks.shape[widest], pieces), axis=widest)  9.65 us
    all_to_all x1, blocking collectives, shards(): lax.all_to_all(jnp.stack([lax.all_to_all(own_columns, 'expert', split_axi...  6.91 us
    reduce_sum x1, other arithmetic, sent_and_summed(): return arrived.sum(axis=0)  6.28 us
  transfers between devices with their start and end apart: 3, of which 3 were waited for; matrix products, arithmetic and copies ran while one was open for 5% of the time, Pallas kernels for 0%

profile of v1, /device:TPU:640, one launch (start us, length us, event | category | flops | bytes accessed | tf_op | source)
XLA Modules:
  0.0 300.3 jit_solution(3893910572671750895)
XLA Ops:
  0.0 0.0 copy-start
  0.0 0.9 copy.87
  0.9 0.1 eq.29
  1.0 0.1 fusion.12
  1.1 0.2 select_reduce_fusion.1
  1.3 0.1 reshape.54
  1.4 0.1 copy.89
  1.5 0.1 fusion.11
  1.5 1.9 convolution_convert_fusion
  3.4 1.1 reshape.56
  4.5 0.8 broadcast_in_dim.2
  5.3 2.0 constant_dynamic-slice_fusion
  7.3 21.3 %all-to-all-start = ((bf16[64,5,3072]{2,1,0:T(8,128)(2,1)}), bf16[64,5,3072]{2,1,0:T(8,128)(2,1)}, u32[]{:S(2)}, u32[]{:S(2)}) async-start(bf16[64,5,3072]{2,1,0:T(8,128)(2,1)} %constant_dynamic-slice_fusion), calls=%async_computation | async-start | bytes 6291456 | tf_op jit(solution)/shard_map/all_to_all | solution.py:78
  28.6 4.6 %copy.110 = bf16[6144,256]{1,0:T(8,128)(2,1)} copy(bf16[6144,256]{0,1:T(8,128)(2,1)} %bitcast.50) | data formatting | bytes 6291456 | tf_op jit(solution)/shard_map/dot_general | solution.py:93
  33.2 71.2 %all-to-all-done = bf16[64,5,3072]{2,1,0:T(8,128)(2,1)} async-done(((bf16[64,5,3072]{2,1,0:T(8,128)(2,1)}), bf16[64,5,3072]{2,1,0:T(8,128)(2,1)}, u32[]{:S(2)}, u32[]{:S(2)}) %all-to-all-start) | async-done | bytes 1966112 | tf_op jit(solution)/shard_map/all_to_all | solution.py:78
  104.4 3.2 %copy.116 = bf16[64,5,3072]{2,0,1:T(8,128)(2,1)S(1)} copy(bf16[64,5,3072]{2,1,0:T(8,128)(2,1)} %all-to-all-done) | data formatting | bytes 3932160 | tf_op jit(solution)/shard_map/all_to_all | solution.py:78
  107.5 0.3 pad_maximum_fusion
  107.9 6.9 %all_to_all.25 = bf16[2,64,5,3072]{3,1,2,0:T(8,128)(2,1)S(1)} all-to-all(bf16[2,64,5,3072]{3,1,2,0:T(8,128)(2,1)S(1)} %pad_maximum_fusion), channel_id=1, replica_groups=mesh['groups'=2,'expert'=64,'tensor'=2] {'tensor'}, dimensions={0} | all-to-all | bytes 7864320 | tf_op jit(solution)/shard_map/all_to_all | solution.py:76
  114.8 5.9 %copy.97 = bf16[64,5,2,3072]{3,2,1,0:T(2,128)(2,1)} copy(bf16[64,5,2,3072]{3,0,1,2:T(8,128)(2,1)S(1)} %bitcast.43) | data formatting | bytes 7864320 | tf_op jit(solution)/shard_map/reshape | solution.py:75
  120.7 3.1 %copy.112 = bf16[40,8,2,3072]{3,1,2,0:T(8,128)(2,1)S(1)} copy(bf16[40,8,2,3072]{3,2,1,0:T(2,128)(2,1)} %bitcast.44) | data formatting | bytes 7864320
  123.9 0.0 copy-done
  123.9 0.0 copy-start.5
  123.9 1.2 fusion.2
  125.1 0.6 copy-done.5
  125.8 0.0 copy-start.3
  125.8 1.8 fusion.7
  127.6 1.0 dot_general.24
  128.6 0.0 copy-done.3
  128.6 1.2 convolution_bitcast_fusion
  129.8 0.9 copy.100
  130.8 11.3 %all_to_all.26 = f32[2,64,5,3072]{3,1,2,0:T(8,128)} all-to-all(f32[2,64,5,3072]{3,1,2,0:T(8,128)S(1)} %copy.100), channel_id=1, replica_groups=mesh['groups'=2,'expert'=64,'tensor'=2] {'tensor'}, dimensions={0} | all-to-all | bytes 15728640 | tf_op jit(solution)/shard_map/all_to_all | solution.py:17
  142.1 6.3 %reduce_sum.48 = f32[64,5,3072]{2,0,1:T(8,128)} reduce(f32[2,64,5,3072]{3,1,2,0:T(8,128)} %all_to_all.26, f32[]{:T(128)} %constant.36.clone.1), dimensions={0}, to_apply=%region_6.7 | reduce | flops 983040 | bytes 11796484 | tf_op jit(solution)/shard_map/reduce_sum | solution.py:18
  148.4 1.5 split.8
  150.0 2.4 copy.102
  152.4 31.4 %all-to-all-start.3 = ((f32[64,1,2,3072]{3,2,1,0:T(2,128)}), f32[64,1,2,3072]{3,2,1,0:T(2,128)}, u32[]{:S(2)}, u32[]{:S(2)}) async-start(f32[64,1,2,3072]{3,2,1,0:T(2,128)} %copy.102), calls=%async_computation.3 | async-start | bytes 3145728 | tf_op jit(solution)/shard_map/all_to_all | solution.py:40
  183.8 1.9 split.9
  185.7 3.8 %copy.103 = f32[64,1,3,3072]{3,1,2,0:T(1,128)} copy(f32[64,1,3,3072]{3,0,2,1:T(8,128)S(1)} %split.9) | data formatting | bytes 4718592 | tf_op jit(solution)/shard_map/split | solution.py:38
  189.5 0.0 copy-start.2
  189.5 34.6 %all-to-all-done.3 = f32[64,1,2,3072]{3,2,1,0:T(2,128)} async-done(((f32[64,1,2,3072]{3,2,1,0:T(2,128)}), f32[64,1,2,3072]{3,2,1,0:T(2,128)}, u32[]{:S(2)}, u32[]{:S(2)}) %all-to-all-start.3) | async-done | bytes 1572896 | tf_op jit(solution)/shard_map/all_to_all | solution.py:40
  224.1 9.3 %all-to-all-start.4 = ((f32[64,1,3,3072]{3,1,2,0:T(1,128)}), f32[64,1,3,3072]{3,1,2,0:T(1,128)S(1)}, u32[]{:S(2)}, u32[]{:S(2)}) async-start(f32[64,1,3,3072]{3,1,2,0:T(1,128)} %copy.103), calls=%async_computation.4 | async-start | bytes 4718592 | tf_op jit(solution)/shard_map/all_to_all | solution.py:40
  233.4 0.1 copy.93
  233.5 0.1 copy.94
  233.6 0.1 reshape.61
  233.7 0.0 copy-done.2
  233.7 0.7 gather_fusion
  234.4 0.1 reshape.64
  234.5 0.1 fusion.15
  234.6 0.2 fusion.14
  234.8 0.1 fusion.13
  234.9 0.1 copy.95
  234.9 0.1 select_reduce_fusion
  235.0 3.1 %copy.104 = f32[64,1,2,3072]{3,0,2,1:T(8,128)} copy(f32[64,1,2,3072]{3,2,1,0:T(2,128)} %all-to-all-done.3) | data formatting | bytes 3145728 | tf_op jit(solution)/shard_map/all_to_all | solution.py:40
  238.1 51.2 %all-to-all-done.4 = f32[64,1,3,3072]{3,1,2,0:T(1,128)S(1)} async-done(((f32[64,1,3,3072]{3,1,2,0:T(1,128)}), f32[64,1,3,3072]{3,1,2,0:T(1,128)S(1)}, u32[]{:S(2)}, u32[]{:S(2)}) %all-to-all-start.4) | async-done | bytes 2359328 | tf_op jit(solution)/shard_map/all_to_all | solution.py:40
  289.3 0.0 copy-start.4
  289.3 0.4 copy.105
  289.7 1.0 copy-done.4
  290.7 0.0 copy-start.1
  290.7 2.3 pad_maximum_fusion.1
  293.0 3.6 %reduce_sum.49 = f32[4,5,3072]{2,0,1:T(4,128)} reduce(f32[4,16,5,3072]{3,1,0,2:T(8,128)} %bitcast.42, f32[]{:T(128)} %constant.36.clone.1), dimensions={1}, to_apply=%region_7.8 | reduce | flops 921600 | bytes 4177924 | tf_op jit(solution)/shard_map/reduce_sum | solution.py:98
  296.6 1.1 copy.106
  297.7 0.8 reshape.60
  298.5 1.9 convolution_convert_fusion.1
  300.3 0.0 copy-done.1
  (3 shorter events, 0.1 us)
Async XLA Ops:
  0.0 123.9 %copy-start = (bf16[1,6144,256]{2,1,0:T(8,128)(2,1)S(1)}, bf16[1,6144,256]{2,1,0:T(8,128)(2,1)}, u32[]{:S(2)}) copy-start(bf16[1,6144,256]{2,1,0:T(8,128)(2,1)} %param.9) | copy-start | bytes 9437188
  7.3 97.1 %all-to-all-start = ((bf16[64,5,3072]{2,1,0:T(8,128)(2,1)}), bf16[64,5,3072]{2,1,0:T(8,128)(2,1)}, u32[]{:S(2)}, u32[]{:S(2)}) async-start(bf16[64,5,3072]{2,1,0:T(8,128)(2,1)} %constant_dynamic-slice_fusion), calls=%async_computation | async-start | bytes 6291456 | tf_op jit(solution)/shard_map/all_to_all | solution.py:78
  123.9 1.9 copy-start.5
  125.8 2.8 copy-start.3
  152.4 71.8 %all-to-all-start.3 = ((f32[64,1,2,3072]{3,2,1,0:T(2,128)}), f32[64,1,2,3072]{3,2,1,0:T(2,128)}, u32[]{:S(2)}, u32[]{:S(2)}) async-start(f32[64,1,2,3072]{3,2,1,0:T(2,128)} %copy.102), calls=%async_computation.3 | async-start | bytes 3145728 | tf_op jit(solution)/shard_map/all_to_all | solution.py:40
  189.5 44.2 %copy-start.2 = (f32[8,4]{0,1:T(4,128)S(1)}, f32[8,4]{0,1:T(4,128)}, u32[]{:S(2)}) copy-start(f32[8,4]{0,1:T(4,128)} %param.8) | copy-start | bytes 388
  224.1 65.1 %all-to-all-start.4 = ((f32[64,1,3,3072]{3,1,2,0:T(1,128)}), f32[64,1,3,3072]{3,1,2,0:T(1,128)S(1)}, u32[]{:S(2)}, u32[]{:S(2)}) async-start(f32[64,1,3,3072]{3,1,2,0:T(1,128)} %copy.103), calls=%async_computation.4 | async-start | bytes 4718592 | tf_op jit(solution)/shard_map/all_to_all | solution.py:40
  289.3 1.4 copy-start.4
  290.7 9.6 %copy-start.1 = (bf16[1,6144,256]{2,1,0:T(8,128)(2,1)S(1)}, bf16[1,6144,256]{2,1,0:T(8,128)(2,1)}, u32[]{:S(2)}) copy-start(bf16[1,6144,256]{2,1,0:T(8,128)(2,1)} %param.9) | copy-start | bytes 9437188
